TPU v7x, 32 devices: a whole 2x2x4 slice. The times are simulated.
32 devices in a mesh: groups: 2 (over y), ep: 4 (over z), tp: 2 (over x), dp: 2 (over core).
Axes of the slice: x: 2, y: 2, z: 4, core: 2. Of those that a mesh axis runs over, the one named last changes fastest.
Arguments:
- tokens: bfloat16 [256, 5120], P(('groups', 'ep', 'tp', 'dp')), parts along dimension 0, may hold values from -6 to 6
- route_weights: float32 [256, 8], P(('groups', 'ep', 'tp', 'dp')), parts along dimension 0, may hold values from 0.1 to 1
- expert_ids: int32 [256, 8], P(('groups', 'ep', 'tp', 'dp')), parts along dimension 0, may hold values from 0 to 31, all different within a row; in each aligned block of 8 rows (0 to 7, 8 to 15, ...) at most 4 rows name the same one
- gate_weight: bfloat16 [32, 5120, 1024], P('ep', None, ('tp', 'dp')), may hold values from -0.078125 to 0.078125
- up_weight: bfloat16 [32, 5120, 1024], P('ep', None, ('tp', 'dp')), may hold values from -0.078125 to 0.078125
- down_weight: bfloat16 [32, 1024, 5120], P('ep', None, ('tp', 'dp')), may hold values from -0.1875 to 0.1875
Outputs:
- combined: bfloat16 [256, 5120], P(('groups', 'ep', 'tp', 'dp')), parts along dimension 0
There are 2 independent parts, one for each index of `groups`. A program takes and returns all parts, laid end to end along the dimension named above; an argument that names none is the same for every part. Nothing has to cross between parts.
Inputs may be any that keep to these rules, and one draw needn't show every extreme that they name: `expert_ids`: each row names 8 different experts. Among the 8 rows of one device no expert is named more than 4 times, and in every draw some device's rows name some expert exactly 4 times.
All inputs are finite; a program needn't handle non-finite values.
Results may differ from a plain program's by a relative error of at most 0.0057.
Values may be sent and summed in bfloat16 or wider, within the bound.
No kernel may reach another device: no remote copies, remote signals or barrier semaphores. Data moves between devices by JAX's collectives and lax.ppermute only.
A program may use at most 128 MiB of HBM per device.

v0:
```python
import jax
import jax.numpy as jnp
from jax import lax
from jax.sharding import PartitionSpec as P

CAP = 4


def route_table(ids, experts, capacity):
    tok_count, top_count = ids.shape
    flat = ids.reshape(-1)
    onehot = (flat[:, None] == jnp.arange(experts, dtype=jnp.int32)[None, :]).astype(jnp.int32)
    slots = jnp.sum(onehot * jnp.cumsum(onehot, axis=0), axis=1) - 1
    place = flat * capacity + slots
    owner = jnp.arange(tok_count * top_count, dtype=jnp.int32) // top_count
    table = jnp.full((experts * capacity,), tok_count, jnp.int32).at[place].set(owner)
    return (place, table)


def per_device(tokens, route_weights, expert_ids, gate_weight, up_weight, down_weight):
    n_owner = lax.axis_size("ep")
    tok_count, top_count = expert_ids.shape
    exp_local = gate_weight.shape[0]
    experts = exp_local * n_owner
    width = tokens.shape[1]
    place, table = route_table(expert_ids, experts, CAP)
    sendbuf = jnp.take(tokens, table, axis=0, mode="fill", fill_value=0).reshape(
        experts, CAP, width
    )
    arrived = lax.all_to_all(sendbuf, "ep", split_axis=0, concat_axis=0, tiled=True)
    arrived = arrived.reshape(1, n_owner, exp_local, CAP, width)
    piece = lax.all_gather(arrived, ("tp", "dp"), axis=0, tiled=True)
    gate = jnp.einsum("gsecd,edf->gsecf", piece, gate_weight, preferred_element_type=jnp.float32)
    up = jnp.einsum("gsecd,edf->gsecf", piece, up_weight, preferred_element_type=jnp.float32)
    hidden = (jax.nn.silu(gate) * up).astype(jnp.bfloat16)
    partial_out = jnp.einsum(
        "gsecf,efd->gsecd",
        lax.all_gather(hidden, ("tp", "dp"), axis=4, tiled=True),
        down_weight,
        preferred_element_type=jnp.float32,
    )
    expert_out = partial_out.astype(jnp.bfloat16)
    mine = lax.all_to_all(expert_out, ("tp", "dp"), split_axis=0, concat_axis=4, tiled=True)
    mine = mine.reshape(n_owner * exp_local, CAP, width)
    returned = lax.all_to_all(mine, "ep", split_axis=0, concat_axis=0, tiled=True)
    picked = jnp.take(returned.reshape(experts * CAP, width), place, axis=0)
    picked = picked.reshape(tok_count, top_count, width).astype(jnp.float32)
    combined = jnp.sum(picked * route_weights[:, :, None], axis=1)
    return combined.astype(jnp.bfloat16)


def solution(mesh):
    return jax.shard_map(
        per_device,
        mesh=mesh,
        in_specs=(
            P(("groups", "ep", "tp", "dp"), None),
            P(("groups", "ep", "tp", "dp"), None),
            P(("groups", "ep", "tp", "dp"), None),
            P("ep", None, ("tp", "dp")),
            P("ep", None, ("tp", "dp")),
            P("ep", None, ("tp", "dp")),
        ),
        out_specs=P(("groups", "ep", "tp", "dp"), None),
        check_vma=False,
    )
```

profile of v0, /device:TPU:0, one launch (start us, length us, event | category | flops | bytes accessed | tf_op | source)
XLA Modules:
  0.0 212.0 jit_solution(12040743795864728024)
XLA Ops:
  6.5 0.8 reshape.76
  7.3 0.7 broadcast_multiply_fusion
  8.0 0.1 fusion.24
  8.1 0.1 reduce_window_sum.11
  8.2 0.2 select_reduce_fusion
  8.4 0.1 mul.40
  8.5 0.8 scatter_custom_fusion
  9.3 1.3 gather_fusion
  10.6 0.5 gather.13
  11.1 0.1 broadcast_in_dim.32
  11.3 0.7 broadcast_select_fusion
  11.9 37.5 %all_to_all.25 = bf16[32,4,5120]{2,1,0:T(4,128)(2,1)S(1)} all-to-all(bf16[32,4,5120]{2,1,0:T(4,128)(2,1)S(1)} %broadcast_select_fusion), channel_id=1, replica_groups=mesh['groups'=2,'ep'=4,'tp'=2,'dp'=2] {'ep'}, dimensions={0} | all-to-all | bytes 2621440 | tf_op jit(solution)/shard_map/all_to_all | solution.py:30
  49.4 1.7 copy.13
  51.1 0.0 all-gather.3.cloned.1.call-update
  51.1 0.2 all-gather.5.cloned.1.call-start
  51.3 39.5 %all-gather.3.cloned.1.call-done = bf16[4,4,8,4,5120]{4,3,1,0,2:T(4,128)(2,1)} async-done(((bf16[1,4,8,4,5120]{4,3,1,0,2:T(4,128)(2,1)}), bf16[4,4,8,4,5120]{4,3,1,0,2:T(4,128)(2,1)}) %all-gather.3.cloned.1.call-update) | async-done | bytes 5242896 | tf_op jit(solution)/shard_map/all_gather | solution.py:32
  90.8 13.1 %fusion.12 = f32[4,4,8,4,256]{4,3,1,0,2:T(4,128)S(1)} fusion(bf16[4,4,8,4,5120]{4,3,1,0,2:T(4,128)(2,1)} %all-gather.3.cloned.1.call-done, bf16[8,5120,256]{2,1,0:T(8,128)(2,1)} %param.9), kind=kOutput, calls=%fused_computation.13 | convolution fusion | flops 1342177280 | bytes 26738688 | tf_op jit(solution)/shard_map/gsecd,edf->gsecf/dot_general | solution.py:33
  103.9 12.2 %fusion.21 = bf16[4,4,8,4,256]{4,3,1,0,2:T(4,128)(2,1)} fusion(bf16[4,4,8,4,5120]{4,3,1,0,2:T(4,128)(2,1)S(1)} %copy-done.4, bf16[8,5120,256]{2,1,0:T(8,128)(2,1)} %param.10, f32[4,4,8,4,256]{4,3,1,0,2:T(4,128)S(1)} %fusion.12), kind=kOutput, calls=%fused_computation.16 | convolution fusion | flops 1342963712 | bytes 27000832 | tf_op jit(solution)/shard_map/gsecd,edf->gsecf/dot_general | solution.py:34
  116.1 0.0 all-gather.5.cloned.1.call-update
  116.1 17.0 %all-gather.5.cloned.1.call-done = bf16[4,4,8,4,1024]{4,3,1,0,2:T(4,128)(2,1)} async-done(((bf16[4,4,8,4,256]{4,3,1,0,2:T(4,128)(2,1)}), bf16[4,4,8,4,1024]{4,3,1,0,2:T(4,128)(2,1)}) %all-gather.5.cloned.1.call-update) | async-done | bytes 1048592 | tf_op jit(solution)/shard_map/all_gather | solution.py:38
  133.1 11.3 %fusion.9 = bf16[4,4,8,4,1280]{4,3,1,0,2:T(4,128)(2,1)S(1)} fusion(bf16[4,4,8,4,1024]{4,3,1,0,2:T(4,128)(2,1)} %all-gather.5.cloned.1.call-done, bf16[8,1024,1280]{2,1,0:T(8,128)(2,1)} %param.11), kind=kOutput, calls=%fused_computation.10 | convolution fusion | flops 1342832640 | bytes 23330816 | tf_op jit(solution)/shard_map/gsecf,efd->gsecd/dot_general | solution.py:36
  144.4 0.5 copy.14
  144.9 19.7 %all_to_all.26 = bf16[4,4,8,4,1280]{4,3,1,2,0:T(4,128)(2,1)S(1)} all-to-all(bf16[4,4,8,4,1280]{4,3,1,2,0:T(4,128)(2,1)S(1)} %copy.14), channel_id=1, replica_groups=mesh['groups'=2,'ep'=4,'tp'=2,'dp'=2] {'tp','dp'}, dimensions={0} | all-to-all | bytes 2621440 | tf_op jit(solution)/shard_map/all_to_all | solution.py:43
  164.6 1.0 copy.22
  165.6 1.4 reshape.108
  167.0 4.7 %all-to-all-start.2 = ((bf16[32,4,5120]{2,1,0:T(4,128)(2,1)}), bf16[32,4,5120]{2,1,0:T(4,128)(2,1)S(1)}, u32[]{:S(2)}, u32[]{:S(2)}) async-start(bf16[32,4,5120]{2,1,0:T(4,128)(2,1)} %reshape.108), calls=%async_computation.2 | async-start | bytes 2621440 | tf_op jit(solution)/shard_map/all_to_all | solution.py:45
  171.7 0.1 sub.15
  171.8 30.9 %all-to-all-done.2 = bf16[32,4,5120]{2,1,0:T(4,128)(2,1)S(1)} async-done(((bf16[32,4,5120]{2,1,0:T(4,128)(2,1)}), bf16[32,4,5120]{2,1,0:T(4,128)(2,1)S(1)}, u32[]{:S(2)}, u32[]{:S(2)}) %all-to-all-start.2) | async-done | bytes 1310752 | tf_op jit(solution)/shard_map/all_to_all | solution.py:45
  202.7 0.3 reshape.79
  203.0 0.0 copy-start.3
  203.0 0.9 gather_fusion.1
  204.0 1.2 multiply_reduce_fusion
  (18 shorter events, 0.1 us)
Async XLA Ops:
  6.5 2.8 %copy-start = (bf16[8,5120]{1,0:T(8,128)(2,1)S(1)}, bf16[8,5120]{1,0:T(8,128)(2,1)}, u32[]{:S(2)}) copy-start(bf16[8,5120]{1,0:T(8,128)(2,1)} %param.6) | copy-start | bytes 245764
  6.5 84.3 %all-gather.3.cloned.1.call-start = ((), (), s32[]{:S(2)}) async-start(), calls=%async_computation.3 | async-start | bytes 6553600 | tf_op jit(solution)/shard_map/all_gather | solution.py:32
  51.1 82.0 %all-gather.5.cloned.1.call-start = ((), (), s32[]{:S(2)}) async-start(), calls=%async_computation.4 | async-start | bytes 1310720 | tf_op jit(solution)/shard_map/all_gather | solution.py:38
  90.8 13.1 %copy-start.4 = (bf16[4,4,8,4,5120]{4,3,1,0,2:T(4,128)(2,1)S(1)}, bf16[4,4,8,4,5120]{4,3,1,0,2:T(4,128)(2,1)}, u32[]{:S(2)}) copy-start(bf16[4,4,8,4,5120]{4,3,1,0,2:T(4,128)(2,1)} %all-gather.3.cloned.1.call-done) | copy-start | bytes 15728644
  167.0 4.8 %copy-start.2 = (s32[8,8]{1,0:T(8,128)S(1)}, s32[8,8]{1,0:T(8,128)}, u32[]{:S(2)}) copy-start(s32[8,8]{1,0:T(8,128)} %param.8) | copy-start | bytes 772
  167.0 35.7 %all-to-all-start.2 = ((bf16[32,4,5120]{2,1,0:T(4,128)(2,1)}), bf16[32,4,5120]{2,1,0:T(4,128)(2,1)S(1)}, u32[]{:S(2)}, u32[]{:S(2)}) async-start(bf16[32,4,5120]{2,1,0:T(4,128)(2,1)} %reshape.108), calls=%async_computation.2 | async-start | bytes 2621440 | tf_op jit(solution)/shard_map/all_to_all | solution.py:45
  203.0 1.0 copy-start.3
  203.0 2.1 %copy-start.1 = (bf16[8,5120]{1,0:T(8,128)(2,1)S(1)}, bf16[8,5120]{1,0:T(8,128)(2,1)}, u32[]{:S(2)}) copy-start(bf16[8,5120]{1,0:T(8,128)(2,1)} %param.6) | copy-start | bytes 245764
Sparse Core Ops, SparseCore 0:
  51.2 39.5 all-gather.2
  116.2 16.8 all-gather.4
where the time goes:
time: 212 us
  waiting for transfers between devices  87.3 us (41%)
  blocking collectives  57.2 us (27%)
  matrix products  36.6 us (17%)
  between operations  13.6 us (6%)
  local copies, waits for them, and re-layouts  9.45 us (4%)
  starting transfers between devices  4.95 us (2%)
  other arithmetic  2.91 us (1%)
    all_gather x1, waiting for transfers between devices, per_device(): piece = lax.all_gather(arrived, ('tp', 'dp'), axis=0, tiled=True)  39.5 us
    all_to_all x1, blocking collectives, per_device(): lax.all_to_all(sendbuf, 'ep', split_axis=0, concat_axis=0, tiled=True)  37.5 us
    all_to_all x1, waiting for transfers between devices, per_device(): lax.all_to_all(mine, 'ep', split_axis=0, concat_axis=0, tiled=True)  30.9 us
    all_to_all x1, blocking collectives, per_device(): lax.all_to_all(expert_out, ('tp', 'dp'), split_axis=0, concat_axis=4, til...  19.7 us
    all_gather x1, waiting for transfers between devices, per_device(): lax.all_gather(hidden, ('tp', 'dp'), axis=4, tiled=True)  17 us
    dot_general x1, matrix products, per_device(): jnp.einsum('gsecd,edf->gsecf', piece, gate_weight, preferred_element_type...  13.1 us
    dot_general x1, matrix products, per_device(): jnp.einsum('gsecd,edf->gsecf', piece, up_weight, preferred_element_type=j...  12.2 us
    dot_general x1, matrix products, per_device(): jnp.einsum('gsecf,efd->gsecd', lax.all_gather(hidden, ('tp', 'dp'), axis=...  11.3 us
  transfers between devices with their start and end apart: 3, of which 3 were waited for; matrix products, arithmetic and copies ran while one was open for 0% of the time, Pallas kernels for 0%

commit v1 on v0

--- a/solution.py
+++ b/solution.py
@@ -33,12 +33,41 @@
     gate = jnp.einsum("gsecd,edf->gsecf", piece, gate_weight, preferred_element_type=jnp.float32)
     up = jnp.einsum("gsecd,edf->gsecf", piece, up_weight, preferred_element_type=jnp.float32)
     hidden = (jax.nn.silu(gate) * up).astype(jnp.bfloat16)
+    size, place_2, extent = (
+        lax.axis_size(("tp", "dp")),
+        lax.axis_index(("tp", "dp")),
+        hidden.shape[4],
+    )
+    ahead = [(i, (i + 1) % size) for i in range(size)]
+    backward = [(i, (i - 1) % size) for i in range(size)]
+    half = size // 2
+    from_left = from_right = hidden
     partial_out = jnp.einsum(
         "gsecf,efd->gsecd",
-        lax.all_gather(hidden, ("tp", "dp"), axis=4, tiled=True),
-        down_weight,
+        hidden,
+        lax.dynamic_slice_in_dim(down_weight, place_2 * extent, hidden.shape[4], axis=1),
         preferred_element_type=jnp.float32,
     )
+    for step in range(1, half + 1):
+        from_left = lax.ppermute(from_left, ("tp", "dp"), ahead)
+        if step < size - half:
+            from_right = lax.ppermute(from_right, ("tp", "dp"), backward)
+            partial_out = partial_out + jnp.einsum(
+                "gsecf,efd->gsecd",
+                from_right,
+                lax.dynamic_slice_in_dim(
+                    down_weight, (place_2 + step) % size * extent, from_right.shape[4], axis=1
+                ),
+                preferred_element_type=jnp.float32,
+            )
+        partial_out = partial_out + jnp.einsum(
+            "gsecf,efd->gsecd",
+            from_left,
+            lax.dynamic_slice_in_dim(
+                down_weight, (place_2 - step) % size * extent, from_left.shape[4], axis=1
+            ),
+            preferred_element_type=jnp.float32,
+        )
     expert_out = partial_out.astype(jnp.bfloat16)
     mine = lax.all_to_all(expert_out, ("tp", "dp"), split_axis=0, concat_axis=4, tiled=True)
     mine = mine.reshape(n_owner * exp_local, CAP, width)

time: 212 us -> 202 us (0.953)
  waiting for transfers between devices: 87.3 us -> 73.4 us
    all_gather x1 -> x0, waiting for transfers between devices: 17 us -> none  [per_device(): lax.all_gather(hidden, ('tp', 'dp'), axis=4, tiled=True)]
    ppermute x0 -> x3, waiting for transfers between devices: none -> 2.88 us  [the longest x2 2.87 us: per_device(): from_left = lax.ppermute(from_left, ('tp', 'dp'), ahead)]
    dot_general x1 -> x4, matrix products: 11.3 us -> 13.9 us  [the longest x2 6.83 us: per_device(): jnp.einsum('gsecf,efd->gsecd', from_left, lax.dynamic_slice_in_dim(down_w...]
  transfers between devices with their start and end apart: 3 -> 5, of which waited for: 3 -> 3; matrix products, arithmetic and copies ran while one was open for 0% -> 5% of each run, Pallas kernels for 0% -> 0%
where the time goes in v1:
time: 202 us
  waiting for transfers between devices  73.4 us (36%)
  blocking collectives  57.5 us (28%)
  matrix products  38.5 us (19%)
  between operations  13.7 us (7%)
  local copies, waits for them, and re-layouts  9.42 us (5%)
  starting transfers between devices  6.2 us (3%)
  other arithmetic  2.94 us (1%)
    all_gather x1, waiting for transfers between devices, per_device(): piece = lax.all_gather(arrived, ('tp', 'dp'), axis=0, tiled=True)  39.7 us
    all_to_all x1, blocking collectives, per_device(): lax.all_to_all(sendbuf, 'ep', split_axis=0, concat_axis=0, tiled=True)  37.5 us
    all_to_all x1, waiting for transfers between devices, per_device(): lax.all_to_all(mine, 'ep', split_axis=0, concat_axis=0, tiled=True)  30.9 us
    all_to_all x1, blocking collectives, per_device(): lax.all_to_all(expert_out, ('tp', 'dp'), split_axis=0, concat_axis=4, til...  20 us
    dot_general x1, matrix products, per_device(): jnp.einsum('gsecd,edf->gsecf', piece, gate_weight, preferred_element_type...  13.1 us
    dot_general x1, matrix products, per_device(): jnp.einsum('gsecd,edf->gsecf', piece, up_weight, preferred_element_type=j...  11.5 us
    dot_general x2, matrix products, per_device(): jnp.einsum('gsecf,efd->gsecd', from_left, lax.dynamic_slice_in_dim(down_w...  6.83 us
    all_to_all x1, starting transfers between devices, per_device(): lax.all_to_all(mine, 'ep', split_axis=0, concat_axis=0, tiled=True)  4.39 us
  transfers between devices with their start and end apart: 5, of which 3 were waited for; matrix products, arithmetic and copies ran while one was open for 5% of the time, Pallas kernels for 0%

profile of v1, /device:TPU:0, one launch (start us, length us, event | category | flops | bytes accessed | tf_op | source)
XLA Modules:
  0.0 201.7 jit_solution(151588689759469222)
XLA Ops:
  6.5 0.7 broadcast_multiply_fusion
  7.3 0.8 reshape.76
  8.0 0.1 mul.57
  8.2 0.1 reduce_window_sum.11
  8.3 0.2 select_reduce_fusion
  8.5 0.8 scatter_custom_fusion
  9.3 1.3 gather_fusion
  10.6 0.5 gather.13
  11.1 0.1 broadcast_in_dim.32
  11.3 0.7 broadcast_select_fusion
  11.9 37.5 %all_to_all.25 = bf16[32,4,5120]{2,1,0:T(4,128)(2,1)S(1)} all-to-all(bf16[32,4,5120]{2,1,0:T(4,128)(2,1)S(1)} %broadcast_select_fusion), channel_id=1, replica_groups=mesh['groups'=2,'ep'=4,'tp'=2,'dp'=2] {'ep'}, dimensions={0} | all-to-all | bytes 2621440 | tf_op jit(solution)/shard_map/all_to_all | solution.py:30
  49.4 1.7 copy.13
  51.2 39.7 %all-gather.2.cloned.1.call-done = bf16[4,4,8,4,5120]{4,3,1,0,2:T(4,128)(2,1)} async-done(((bf16[1,4,8,4,5120]{4,3,1,0,2:T(4,128)(2,1)}), bf16[4,4,8,4,5120]{4,3,1,0,2:T(4,128)(2,1)}) %all-gather.2.cloned.1.call-update) | async-done | bytes 5242896 | tf_op jit(solution)/shard_map/all_gather | solution.py:32
  90.8 13.1 %fusion.31 = f32[4,4,8,4,256]{4,3,1,0,2:T(4,128)S(1)} fusion(bf16[4,4,8,4,5120]{4,3,1,0,2:T(4,128)(2,1)} %all-gather.2.cloned.1.call-done, bf16[8,5120,256]{2,1,0:T(8,128)(2,1)} %param.9), kind=kOutput, calls=%fused_computation.26 | convolution fusion | flops 1342177280 | bytes 26738688 | tf_op jit(solution)/shard_map/gsecd,edf->gsecf/dot_general | solution.py:33
  103.9 11.5 %fusion.40 = bf16[4,4,8,4,256]{4,3,1,0,2:T(4,128)(2,1)S(1)} fusion(bf16[4,4,8,4,5120]{4,3,1,0,2:T(4,128)(2,1)S(1)} %copy-done.4, bf16[8,5120,256]{2,1,0:T(8,128)(2,1)} %param.10, f32[4,4,8,4,256]{4,3,1,0,2:T(4,128)S(1)} %fusion.31), kind=kOutput, calls=%fused_computation.29 | convolution fusion | flops 1342963712 | bytes 27000832 | tf_op jit(solution)/shard_map/gsecd,edf->gsecf/dot_general | solution.py:34
  115.4 0.3 collective-permute-start.1
  115.7 1.5 collective-permute-start
  117.2 3.3 %fusion.10 = f32[8,1280,4,4,4]{1,4,3,2,0:T(4,128)S(1)} fusion(bf16[4,4,8,4,256]{4,3,1,0,2:T(4,128)(2,1)S(1)} %fusion.40, bf16[8,1024,1280]{2,1,0:T(8,128)(2,1)} %param.11, s32[]{:T(128)S(6)} %select_n.65), kind=kOutput, calls=%fused_computation.13 | convolution fusion | flops 335544320 | bytes 8126468 | tf_op jit(solution)/shard_map/gsecf,efd->gsecd/dot_general | solution.py:45
  120.5 2.9 %collective-permute-done.1 = bf16[4,4,8,4,256]{4,3,1,0,2:T(4,128)(2,1)S(1)} collective-permute-done((bf16[4,4,8,4,256]{4,3,1,0,2:T(4,128)(2,1)S(1)}, bf16[4,4,8,4,256]{4,3,1,0,2:T(4,128)(2,1)S(1)}, u32[]{:S(2)}, u32[]{:S(2)}) %collective-permute-start.1) | collective-permute-done | bytes 262176 | tf_op jit(solution)/shard_map/ppermute | solution.py:52
  123.4 3.3 %fusion.6 = f32[8,1280,4,4,4]{1,4,3,2,0:T(4,128)S(1)} fusion(bf16[4,4,8,4,256]{4,3,1,0,2:T(4,128)(2,1)S(1)} %collective-permute-done.1, bf16[8,1024,1280]{2,1,0:T(8,128)(2,1)} %param.11, s32[]{:T(128)S(6)} %select_n.73), kind=kOutput, calls=%fused_computation.9 | convolution fusion | flops 335544320 | bytes 8126468 | tf_op jit(solution)/shard_map/gsecf,efd->gsecd/dot_general | solution.py:63
  126.8 3.8 %fusion.19 = f32[8,1280,4,4,4]{1,4,3,2,0:T(4,128)S(1)} fusion(f32[8,1280,4,4,4]{1,4,3,2,0:T(4,128)S(1)} %fusion.6, f32[8,1280,4,4,4]{1,4,3,2,0:T(4,128)S(1)} %fusion.10, bf16[4,4,8,4,256]{4,3,1,0,2:T(4,128)(2,1)S(1)} %collective-permute-done, bf16[8,1024,1280]{2,1,0:T(8,128)(2,1)} %param.11, s32[]{:T(128)S(6)} %select_n.71), kind=kOutput, calls=%fused_computation.20 | convolution fusion | flops 336855040 | bytes 13369348 | tf_op jit(solution)/shard_map/gsecf,efd->gsecd/dot_general | solution.py:55
  130.5 3.5 %fusion.28 = bf16[4,4,8,4,1280]{4,3,1,0,2:T(4,128)(2,1)S(1)} fusion(f32[8,1280,4,4,4]{1,4,3,2,0:T(4,128)S(1)} %fusion.19, bf16[4,4,8,4,256]{4,3,1,0,2:T(4,128)(2,1)S(1)} %collective-permute-done.2, bf16[8,1024,1280]{2,1,0:T(8,128)(2,1)} %param.11, s32[]{:T(128)S(6)} %select_n.75), kind=kOutput, calls=%fused_computation.23 | convolution fusion | flops 336855040 | bytes 9437188 | tf_op jit(solution)/shard_map/gsecf,efd->gsecd/dot_general | solution.py:63
  134.0 0.5 copy.14
  134.5 20.0 %all_to_all.26 = bf16[4,4,8,4,1280]{4,3,1,2,0:T(4,128)(2,1)S(1)} all-to-all(bf16[4,4,8,4,1280]{4,3,1,2,0:T(4,128)(2,1)S(1)} %copy.14), channel_id=1, replica_groups=mesh['groups'=2,'ep'=4,'tp'=2,'dp'=2] {'tp','dp'}, dimensions={0} | all-to-all | bytes 2621440 | tf_op jit(solution)/shard_map/all_to_all | solution.py:72
  154.6 1.0 copy.25
  155.6 1.4 reshape.111
  157.0 4.4 %all-to-all-start.2 = ((bf16[32,4,5120]{2,1,0:T(4,128)(2,1)}), bf16[32,4,5120]{2,1,0:T(4,128)(2,1)S(1)}, u32[]{:S(2)}, u32[]{:S(2)}) async-start(bf16[32,4,5120]{2,1,0:T(4,128)(2,1)} %reshape.111), calls=%async_computation.2 | async-start | bytes 2621440 | tf_op jit(solution)/shard_map/all_to_all | solution.py:74
  161.4 0.1 sub.21
  161.5 30.9 %all-to-all-done.2 = bf16[32,4,5120]{2,1,0:T(4,128)(2,1)S(1)} async-done(((bf16[32,4,5120]{2,1,0:T(4,128)(2,1)}), bf16[32,4,5120]{2,1,0:T(4,128)(2,1)S(1)}, u32[]{:S(2)}, u32[]{:S(2)}) %all-to-all-start.2) | async-done | bytes 1310752 | tf_op jit(solution)/shard_map/all_to_all | solution.py:74
  192.4 0.3 reshape.79
  192.7 0.9 gather_fusion.1
  193.6 1.2 multiply_reduce_fusion
  (24 shorter events, 0.2 us)
Async XLA Ops:
  6.5 2.8 %copy-start = (bf16[8,5120]{1,0:T(8,128)(2,1)S(1)}, bf16[8,5120]{1,0:T(8,128)(2,1)}, u32[]{:S(2)}) copy-start(bf16[8,5120]{1,0:T(8,128)(2,1)} %param.6) | copy-start | bytes 245764
  6.5 84.3 %all-gather.2.cloned.1.call-start = ((), (), s32[]{:S(2)}) async-start(), calls=%async_computation.3 | async-start | bytes 6553600 | tf_op jit(solution)/shard_map/all_gather | solution.py:32
  90.8 13.1 %copy-start.4 = (bf16[4,4,8,4,5120]{4,3,1,0,2:T(4,128)(2,1)S(1)}, bf16[4,4,8,4,5120]{4,3,1,0,2:T(4,128)(2,1)}, u32[]{:S(2)}) copy-start(bf16[4,4,8,4,5120]{4,3,1,0,2:T(4,128)(2,1)} %all-gather.2.cloned.1.call-done) | copy-start | bytes 15728644
  115.4 8.0 %collective-permute-start.1 = (bf16[4,4,8,4,256]{4,3,1,0,2:T(4,128)(2,1)S(1)}, bf16[4,4,8,4,256]{4,3,1,0,2:T(4,128)(2,1)S(1)}, u32[]{:S(2)}, u32[]{:S(2)}) collective-permute-start(bf16[4,4,8,4,256]{4,3,1,0,2:T(4,128)(2,1)S(1)} %fusion.40), channel_id=1, source_target_pairs={{0,1},{1,2},{2,3},{3,0},{4,5},{5,6},{6,7},{7,4},{8,9},{9,10},{10,1... | collective-permute-start | bytes 786440 | tf_op jit(solution)/shard_map/ppermute | solution.py:52
  115.7 11.1 %collective-permute-start = (bf16[4,4,8,4,256]{4,3,1,0,2:T(4,128)(2,1)S(1)}, bf16[4,4,8,4,256]{4,3,1,0,2:T(4,128)(2,1)S(1)}, u32[]{:S(2)}, u32[]{:S(2)}) collective-permute-start(bf16[4,4,8,4,256]{4,3,1,0,2:T(4,128)(2,1)S(1)} %fusion.40), channel_id=1, source_target_pairs={{0,3},{1,0},{2,1},{3,2},{4,7},{5,4},{6,5},{7,6},{8,11},{9,8},{10,9... | collective-permute-start | bytes 786440 | tf_op jit(solution)/shard_map/ppermute | solution.py:54
  123.4 7.1 %collective-permute-start.2 = (bf16[4,4,8,4,256]{4,3,1,0,2:T(4,128)(2,1)S(1)}, bf16[4,4,8,4,256]{4,3,1,0,2:T(4,128)(2,1)S(1)}, u32[]{:S(2)}, u32[]{:S(2)}) collective-permute-start(bf16[4,4,8,4,256]{4,3,1,0,2:T(4,128)(2,1)S(1)} %collective-permute-done.1), channel_id=1, source_target_pairs={{0,1},{1,2},{2,3},{3,0},{4,5},{5,6},{6,7},{7,4},{8,9},{9,10},{10,1... | collective-permute-start | bytes 786440 | tf_op jit(solution)/shard_map/ppermute | solution.py:52
  155.6 5.9 %copy-start.2 = (s32[8,8]{1,0:T(8,128)S(1)}, s32[8,8]{1,0:T(8,128)}, u32[]{:S(2)}) copy-start(s32[8,8]{1,0:T(8,128)} %param.8) | copy-start | bytes 772
  157.0 35.4 %all-to-all-start.2 = ((bf16[32,4,5120]{2,1,0:T(4,128)(2,1)}), bf16[32,4,5120]{2,1,0:T(4,128)(2,1)S(1)}, u32[]{:S(2)}, u32[]{:S(2)}) async-start(bf16[32,4,5120]{2,1,0:T(4,128)(2,1)} %reshape.111), calls=%async_computation.2 | async-start | bytes 2621440 | tf_op jit(solution)/shard_map/all_to_all | solution.py:74
  192.4 2.5 %copy-start.1 = (bf16[8,5120]{1,0:T(8,128)(2,1)S(1)}, bf16[8,5120]{1,0:T(8,128)(2,1)}, u32[]{:S(2)}) copy-start(bf16[8,5120]{1,0:T(8,128)(2,1)} %param.6) | copy-start | bytes 245764
  192.7 0.9 copy-start.3
Sparse Core Ops, SparseCore 0:
  51.2 39.5 all-gather.1
